TPU v7x, 256 devices: a whole 4x4x8 slice. The times are simulated.
256 devices in a mesh: rep: 16 (over z_hi, x), tp: 16 (over z_lo, y, core).
Axes of the slice: x: 4, y: 4, z: 8 (z_hi: 4, z_lo: 2; z = z_hi * 2 + z_lo), core: 2. Of those that a mesh axis runs over, the one named last changes fastest.
Arguments:
- tokens: bfloat16 [512, 4096], P(('rep', 'tp')), may hold values from -6 to 6
- conv_state: bfloat16 [3, 512, 8192], P(None, 'rep', 'tp'), may hold values from -6 to 6
- ssm_state: float32 [512, 16, 8192], P('rep', None, 'tp'), may hold values from -6 to 6
- norm_gains: bfloat16 [2, 4096], P(None, ('rep', 'tp')), may hold values from 0.5 to 1.5
- conv_weight: bfloat16 [4, 8192], P(None, ('rep', 'tp')), may hold values from -3 to 3
- conv_skip: bfloat16 [2, 8192], P(None, ('rep', 'tp')), may hold values from -3 to 3
- step_bias: bfloat16 [8192], P(('rep', 'tp')), may hold values from -5 to -1
- decay_log: bfloat16 [16, 8192], P(None, ('rep', 'tp')), may hold values from 0 to 2.796875
- input_proj: bfloat16 [4096, 2, 8192], P(('rep', 'tp')), may hold values from -0.09375 to 0.09375
- select_proj: bfloat16 [8192, 288], P('tp', 'rep'), may hold values from -0.0625 to 0.0625
- step_proj: bfloat16 [256, 8192], P(('rep', 'tp')), may hold values from -0.375 to 0.375
- output_proj: bfloat16 [8192, 4096], P(None, ('rep', 'tp')), may hold values from -0.0625 to 0.0625
- router: bfloat16 [4096, 16], P(('rep', 'tp')), may hold values from -0.09375 to 0.09375
- expert_proj: bfloat16 [4096, 2, 2, 12288], P(('rep', 'tp')), may hold values from -0.09375 to 0.09375
- expert_ids: int32 [512, 2], P(('rep', 'tp')), may hold values from 0 to 15, as said below
Outputs:
- mamba_out: bfloat16 [512, 4096], P(('rep', 'tp'))
- conv_next: bfloat16 [3, 512, 8192], P(None, 'rep', 'tp')
- ssm_next: float32 [512, 16, 8192], P('rep', None, 'tp')
- expert_hidden: bfloat16 [1024, 12288], P('rep', 'tp')
Inputs may be any that keep to these rules, and one draw needn't show every extreme that they name: `expert_ids`: each row names two different experts. Within each aligned block of 2 rows (the rows of one device) each expert e < 2 is named by at most 2 rows.
All inputs are finite; a program needn't handle non-finite values.
Results may differ from a plain program's by a relative error of at most 0.04.
Values may be sent and summed in bfloat16 or wider, within the bound.
A program may use at most 128 MiB of HBM per device.

v0:
```python
import math
import jax
import jax.numpy as jnp
from jax import lax
from jax.sharding import Mesh
from jax.sharding import PartitionSpec as P

CAPACITY = 2
REP_TP = ("rep_0", "rep_1", "tp")
REP = ("rep_0", "rep_1")
epsilon = 1e-05


def in_one_piece(arrays, axis, dim, along):
    widths = [a.shape[along] for a in arrays]
    both = jnp.concatenate(arrays, axis=along)
    out = lax.all_gather(both, axis, axis=dim, tiled=True)
    return tuple(jnp.split(out, [sum(widths[:k]) for k in range(1, len(widths))], axis=along))


def from_everyone(array, axis):
    devices = lax.axis_size(axis)
    return lax.all_to_all(
        jnp.broadcast_to(array[None], (devices, *array.shape)), axis, 0, 0, tiled=True
    )


def joined_along(blocks, dim):
    dims = list(blocks.shape[1:])
    dims[dim] *= blocks.shape[0]
    return jnp.moveaxis(blocks, 0, dim).reshape(dims)


def gathered_copies(array, axis, dim):
    blocks = from_everyone(array, axis)
    return joined_along(blocks, dim)


def gather_packed(arrays, axis, dims):
    ravelled = jnp.concatenate([a.reshape(-1) for a in arrays])
    lines, at, outs = (lax.all_gather(ravelled, axis), 0, [])
    for a, dim in zip(arrays, dims):
        blocks = lines[:, at : at + a.size].reshape(-1, *a.shape)
        outs.append(joined_along(blocks, dim))
        at += a.size
    return tuple(outs)


def over_copies(array, axis):
    return from_everyone(array, axis).astype(jnp.float32).sum(axis=0)


def split_up(array, dim, devices):
    before, after = (array.shape[:dim], array.shape[dim + 1 :])
    return jnp.moveaxis(array.reshape(*before, devices, -1, *after), dim, 0)


def sent_and_summed(array, axis, dim):
    devices = lax.axis_size(axis)
    blocks = lax.all_to_all(split_up(array, dim, devices), axis, 0, 0, tiled=True)
    return jnp.sum(blocks.astype(jnp.float32), axis=0)


def side_by_side(arrays, axis, dim, along):
    widths = [math.prod(a.shape[along:]) for a in arrays]
    both = jnp.concatenate(
        [a.reshape(*a.shape[:along], w) for a, w in zip(arrays, widths)], axis=along
    )
    out = lax.all_gather(both, axis, axis=dim, tiled=True)
    blocks = jnp.split(out, [sum(widths[:k]) for k in range(1, len(widths))], axis=along)
    return tuple((b.reshape(*out.shape[:along], *a.shape[along:]) for a, b in zip(arrays, blocks)))


def own_block(blocks, axes, order):
    dims = [lax.axis_size(a) for a in axes]
    blocks = blocks.reshape(*dims, *blocks.shape[1:])
    blocks = blocks.transpose(*order, *range(len(axes), blocks.ndim))
    blocks = blocks.reshape(-1, *blocks.shape[len(axes) :])
    for k in order:
        blocks = lax.psum_scatter(blocks, axes[k], scatter_dimension=0, tiled=True)
    return blocks[0]


def scatter_axes(array, axes, order, dim):
    devices = lax.axis_size(axes)
    return own_block(split_up(array, dim, devices), axes, order)


def norm_scale(values, gain):
    mean_square = jnp.mean(values * values, axis=-1, keepdims=True)
    return values * lax.rsqrt(mean_square + epsilon) * gain.astype(jnp.float32)


def shards(
    tokens,
    conv_state,
    ssm_state,
    norm_gains,
    conv_weight,
    conv_skip,
    step_bias,
    decay_log,
    input_proj,
    select_proj,
    step_proj,
    output_proj,
    router,
    expert_proj,
    expert_ids,
):
    tp_count = lax.axis_size("tp")
    tp_index = lax.axis_index("tp")
    norm_gain, conv_taps, skip_rows, shift_full, decay_full, router_full = (
        lax.all_gather(norm_gains, REP_TP, axis=1, tiled=True),
        *in_one_piece((conv_weight, conv_skip), REP_TP, 1, 0),
        lax.all_gather(step_bias, REP_TP, axis=0, tiled=True),
        lax.all_gather(decay_log, REP_TP, axis=1, tiled=True),
        lax.all_gather(router, REP_TP, axis=0, tiled=True),
    )
    inner_dev = ssm_state.shape[2]
    channel_start = tp_index * inner_dev
    conv_taps = lax.dynamic_slice_in_dim(conv_taps, channel_start, inner_dev, 1).astype(jnp.float32)
    skip_rows = lax.dynamic_slice_in_dim(skip_rows, channel_start, inner_dev, 1).astype(jnp.float32)
    shift_dev = lax.dynamic_slice_in_dim(shift_full, channel_start, inner_dev, 0).astype(
        jnp.float32
    )
    decay_dev = lax.dynamic_slice_in_dim(decay_full, channel_start, inner_dev, 1).astype(
        jnp.float32
    )
    model_rows = input_proj.shape[0]
    inner_all = input_proj.shape[2]
    input_blocks, expert_blocks, step_blocks = (
        lax.all_to_all(
            input_proj.reshape(model_rows, 1, 2, inner_all),
            "tp",
            split_axis=3,
            concat_axis=0,
            tiled=True,
        ),
        lax.all_to_all(expert_proj, "tp", split_axis=3, concat_axis=0, tiled=True),
        lax.all_to_all(
            step_proj.reshape(step_proj.shape[0], 1, 1, inner_all),
            "tp",
            split_axis=3,
            concat_axis=0,
            tiled=True,
        ),
    )
    output_blocks = lax.all_to_all(output_proj, "tp", split_axis=0, concat_axis=1, tiled=True)
    residual_in = tokens.astype(jnp.float32)
    normed = norm_scale(residual_in, norm_gain[0]).astype(jnp.bfloat16)
    features = gathered_copies(normed, "tp", 0)
    shard_piece = lax.all_gather(input_blocks, REP, axis=0, tiled=True)
    piece_rows = shard_piece.shape[0]
    projected = jnp.dot(
        features, shard_piece.reshape(piece_rows, 2 * inner_dev), preferred_element_type=jnp.float32
    )
    output_rows, step_rows, select_rows = gather_packed(
        (output_blocks, step_blocks, select_proj), REP, (1, 0, 1)
    )
    step_rows = step_rows.reshape(step_rows.shape[0], inner_dev)
    step_rank = step_rows.shape[0]
    state_count = ssm_state.shape[1]
    conv_input = projected[:, :inner_dev]
    gate_z = projected[:, inner_dev:]
    history = conv_state.astype(jnp.float32)
    conv_mix = (
        jnp.sum(conv_taps[:-1, None, :] * history, axis=0)
        + conv_taps[-1] * conv_input
        + skip_rows[0]
    )
    conv_next = jnp.concatenate([conv_state[1:], conv_input.astype(jnp.bfloat16)[None]], axis=0)
    activated = jax.nn.silu(conv_mix)
    select_part = jnp.dot(
        activated.astype(jnp.bfloat16), select_rows, preferred_element_type=jnp.float32
    )
    selected = over_copies(select_part.astype(jnp.bfloat16), "tp").astype(jnp.float32)
    step_low = selected[:, :step_rank].astype(jnp.bfloat16)
    input_map = selected[:, step_rank : step_rank + state_count]
    output_map = selected[:, step_rank + state_count :]
    step_size = jax.nn.softplus(
        jnp.dot(step_low, step_rows, preferred_element_type=jnp.float32) + shift_dev
    )
    decay_rate = -jnp.exp(decay_dev)
    factor = jnp.exp(step_size[:, None, :] * decay_rate[None])
    ssm_next = factor * ssm_state + (step_size * activated)[:, None, :] * input_map[:, :, None]
    readout = jnp.sum(ssm_next * output_map[:, :, None], axis=1) + skip_rows[1] * activated
    gated_out = (readout * jax.nn.silu(gate_z)).astype(jnp.bfloat16)
    output_part = jnp.dot(gated_out, output_rows, preferred_element_type=jnp.float32)
    mixer_out = sent_and_summed(output_part.astype(jnp.bfloat16), "tp", 0)
    residual = residual_in + mixer_out
    mamba_out = residual.astype(jnp.bfloat16)
    moe_in = norm_scale(residual, norm_gain[1]).astype(jnp.bfloat16)
    logits = jnp.dot(moe_in, router_full, preferred_element_type=jnp.float32)
    expert_total = logits.shape[1]
    choose = (
        expert_ids[:, :, None] == jnp.arange(expert_total, dtype=jnp.int32)[None, None, :]
    ).astype(jnp.float32)
    picked = jnp.sum(choose * logits[:, None, :], axis=2)
    first_gate = jax.nn.sigmoid(picked[:, 0] - picked[:, 1])
    second_gate = jax.nn.sigmoid(picked[:, 1] - picked[:, 0])
    window_count = expert_blocks.shape[1]
    window = jnp.arange(window_count, dtype=jnp.int32)
    names_first = expert_ids[:, 0:1] == window[None, :]
    names_second = expert_ids[:, 1:2] == window[None, :]
    zero = jnp.zeros((), jnp.float32)
    gate_w = jnp.where(names_first, first_gate[:, None], zero) + jnp.where(
        names_second, second_gate[:, None], zero
    )
    routed = (names_first | names_second).astype(jnp.int32)
    position = jnp.cumsum(routed, axis=0) - routed
    slot_of = (position[:, :, None] == jnp.arange(CAPACITY, dtype=jnp.int32)[None, None, :]) & (
        routed[:, :, None] > 0
    )
    slot_x = jnp.einsum(
        "tec,td->ecd", slot_of.astype(jnp.bfloat16), moe_in, preferred_element_type=jnp.float32
    )
    slot_local = window_count * CAPACITY
    slot_x = slot_x.astype(jnp.bfloat16).reshape(slot_local, moe_in.shape[1])
    slot_gate = (
        jnp.einsum("tec,te->ec", slot_of.astype(jnp.float32), gate_w)
        .astype(jnp.bfloat16)
        .reshape(slot_local)
    )
    feature_rows = expert_blocks.shape[0]
    replica_rows, gate_all = side_by_side((slot_x, slot_gate), "tp", 0, 1)
    gathered = lax.all_to_all(replica_rows, REP, split_axis=1, concat_axis=0, tiled=True)
    hidden_dev = expert_blocks.shape[3]
    group_rows = tp_count * slot_local
    picked_rows = gathered
    picked_rows = picked_rows.reshape(
        group_rows * lax.axis_size(REP) // slot_local, window_count, CAPACITY, feature_rows
    )
    product = jnp.einsum(
        "gecd,dexf->gecxf", picked_rows, expert_blocks, preferred_element_type=jnp.float32
    )
    summed = scatter_axes(
        product.reshape(group_rows * lax.axis_size(REP), 2 * hidden_dev).astype(jnp.bfloat16),
        REP,
        (1, 0),
        0,
    ).astype(jnp.float32)
    hidden = (
        gate_all.astype(jnp.float32)[:, None]
        * jax.nn.silu(summed[:, :hidden_dev])
        * summed[:, hidden_dev:]
    )
    expert_hidden = hidden.astype(jnp.bfloat16)
    return (mamba_out, conv_next, ssm_next, expert_hidden)


def solution(mesh):
    split = Mesh(mesh.devices.reshape(4, 4, mesh.shape["tp"]), ("rep_0", "rep_1", "tp"))
    return jax.shard_map(
        shards,
        mesh=split,
        in_specs=(
            P(REP_TP, None),
            P(None, REP, "tp"),
            P(REP, None, "tp"),
            P(None, REP_TP),
            P(None, REP_TP),
            P(None, REP_TP),
            P(REP_TP),
            P(None, REP_TP),
            P(REP_TP, None, None),
            P("tp", REP),
            P(REP_TP, None),
            P(None, REP_TP),
            P(REP_TP, None),
            P(REP_TP, None, None, None),
            P(REP_TP, None),
        ),
        out_specs=(P(REP_TP, None), P(None, REP, "tp"), P(REP, None, "tp"), P(REP, "tp")),
        check_vma=False,
    )
```

profile of v0, /device:TPU:2, one launch (start us, length us, event | category | flops | bytes accessed | tf_op | source)
XLA Modules:
  0.0 1973.0 jit_solution(4106802272947335639)
XLA Ops:
  7.2 8.3 copy.135
  16.0 62.6 %reduce.12 = bf16[8192]{0:T(1024)(128)(2,1)S(1)} reduce(bf16[8192,1,1,1]{3,2,1,0:T(2,128)(2,1)} %bitcast.104, bf16[]{:T(256)} %broadcast.160), dimensions={1,2,3}, to_apply=%bitcast.77.reduce_sub_computation | reduce | bytes 32770
  79.2 5.9 all-to-all-start.3
  86.2 5.0 all-to-all-done.3
  91.2 3.5 all-to-all-start.2
  95.0 8.4 reshape.274
  103.4 62.0 %bitcast_reduce_fusion = bf16[8192]{0:T(1024)(128)(2,1)S(1)} fusion(bf16[8192,1,1,1]{3,2,1,0:T(2,128)(2,1)} %reshape.274), kind=kLoop, calls=%fused_computation.72 | loop fusion | bytes 32768 | tf_op jit(solution)/shard_map/all_to_all | solution.py:141
  165.4 2.0 copy.134
  167.4 1.3 reshape.235
  169.6 6.8 copy.129
  176.3 7.7 bitcast_bitcast_fusion
  184.0 5.8 reshape.275
  189.8 18.9 all_to_all.92
  208.7 4.1 reshape.276
  212.8 10.3 copy.152
  223.2 333.4 %all-gather.2 = bf16[256,16,2]{1,2,0:T(2,128)(2,1)S(1)} all-gather(bf16[1,16,2]{1,2,0:T(2,128)(2,1)S(1)} %bitcast.128), channel_id=1, replica_groups=mesh['rep_0'=4,'rep_1'=4,'tp'=16] {'rep_0','rep_1','tp'}, dimensions={0}, use_global_device_ids=true | all-gather | bytes 16448 | tf_op jit(solution)/shard_map/all_gather | solution.py:114
  558.0 3.5 all-to-all-start
  561.5 342.0 %all-gather.1 = bf16[256,32,6]{1,2,0:T(8,128)(2,1)S(1)} all-gather(bf16[1,32,6]{1,2,0:T(8,128)(2,1)S(1)} %maximum_bitcast_fusion.1), channel_id=1, replica_groups=mesh['rep_0'=4,'rep_1'=4,'tp'=16] {'rep_0','rep_1','tp'}, dimensions={0}, use_global_device_ids=true | all-gather | bytes 98688 | tf_op jit(solution)/shard_map/all_gather | solution.py:17
  904.3 5.1 reshape.251
  909.4 1.0 slice.98
  910.4 5.1 reshape.239
  916.6 11.3 copy.132
  927.9 6.0 fusion.24
  934.9 3.6 all-to-all-start.4
  938.5 344.1 %all-gather.3 = bf16[256,32,16]{1,2,0:T(8,128)(2,1)S(1)} all-gather(bf16[1,32,16]{1,2,0:T(8,128)(2,1)S(1)} %bitcast.126), channel_id=1, replica_groups=mesh['rep_0'=4,'rep_1'=4,'tp'=16] {'rep_0','rep_1','tp'}, dimensions={0}, use_global_device_ids=true | all-gather | bytes 263168 | tf_op jit(solution)/shard_map/all_gather | solution.py:117
  1282.9 1.1 reshape.259
  1284.3 98.4 %all-reduce = bf16[8192]{0:T(1024)(128)(2,1)S(1)} all-reduce(bf16[8192]{0:T(1024)(128)(2,1)S(1)} %dynamic-update-slice), channel_id=1, replica_groups=mesh['rep_0'=4,'rep_1'=4,'tp'=16] {'rep_0','rep_1','tp'}, use_global_device_ids=true, to_apply=%add | all-reduce | flops 8192 | bytes 32768
  1382.9 4.4 slice.105
  1387.5 5.1 copy.157
  1392.6 6.5 copy.139
  1399.5 1.4 multiply_reduce_fusion
  1400.9 3.5 convolution_convert_fusion
  1405.3 5.3 all-to-all-start.5
  1410.8 20.2 %copy.142 = bf16[16,2,2,12288]{0,2,1,3:T(2,128)(2,1)} copy(bf16[16,2,2,12288]{3,2,1,0:T(2,128)(2,1)S(1)} %copy-done.1) | data formatting | bytes 3145728 | tf_op args[13]
  1430.9 17.7 reshape.277
  1448.6 328.0 %all_gather.34 = bf16[4096,16]{1,0:T(8,128)(2,1)S(1)} all-gather(bf16[16,16]{1,0:T(8,128)(2,1)S(1)} %copy-done.10), channel_id=1, replica_groups=mesh['rep_0'=4,'rep_1'=4,'tp'=16] {'rep_0','rep_1','tp'}, dimensions={0}, use_global_device_ids=true | all-gather | bytes 131584 | tf_op jit(solution)/shard_map/all_gather | solution.py:118
  1776.6 3.9 all-to-all-start.7
  1782.5 32.2 %all-gather.4 = bf16[16,4,4097]{2,1,0:T(4,128)(2,1)S(1)} all-gather(bf16[1,4,4097]{2,1,0:T(4,128)(2,1)S(1)} %maximum_bitcast_fusion), channel_id=1, replica_groups=mesh['rep_0'=4,'rep_1'=4,'tp'=16] {'tp'}, dimensions={0}, use_global_device_ids=true | all-gather | bytes 557192 | tf_op jit(solution)/shard_map/all_gather | solution.py:69
  1816.0 25.0 %all-to-all-start.6 = ((bf16[64,16,256]{2,0,1:T(8,128)(2,1)}), bf16[64,16,256]{2,0,1:T(8,128)(2,1)S(1)}, u32[]{:S(2)}, u32[]{:S(2)}) async-start(bf16[64,16,256]{2,0,1:T(8,128)(2,1)} %bitcast.95), calls=%async_computation.6 | async-start | bytes 1048576 | tf_op jit(solution)/shard_map/all_to_all | solution.py:227
  1841.1 12.1 reshape.278
  1853.2 26.5 %copy.143 = bf16[16,2,2,16,768]{4,0,3,2,1:T(8,128)(2,1)S(1)} copy(bf16[16,2,2,16,768]{0,2,1,4,3:T(2,128)(2,1)} %bitcast.98) | data formatting | bytes 3145728 | tf_op jit(solution)/shard_map/all_to_all | solution.py:140
  1880.0 1.0 convert_bitcast_fusion
  1880.9 3.2 copy.145
  1884.2 3.3 convert_element_type.118
  1887.5 3.9 copy.146
  1891.5 39.0 %reduce-scatter.3.cloned.1.call-done = bf16[4,64,1536]{2,1,0:T(8,128)(2,1)} async-done(((bf16[16,64,1536]{2,1,0:T(8,128)(2,1)}), bf16[4,64,1536]{2,1,0:T(8,128)(2,1)}) %reduce-scatter.3.cloned.1.call-update) | async-done | bytes 786448 | tf_op jit(solution)/shard_map/reduce_scatter | solution.py:80
  1932.0 32.7 %reduce-scatter.5.cloned.1.call-done = bf16[1,64,1536]{2,1,0:T(8,128)(2,1)} async-done(((bf16[4,64,1536]{2,1,0:T(8,128)(2,1)}), bf16[1,64,1536]{2,1,0:T(8,128)(2,1)}) %reduce-scatter.5.cloned.1.call-update) | async-done | bytes 196624 | tf_op jit(solution)/shard_map/reduce_scatter | solution.py:80
  1964.6 1.0 bitcast_convert_fusion
  (115 shorter events, 15.7 us)
Async XLA Ops:
  7.2 78.0 %copy-start.6 = (bf16[8192,16]{0,1:T(8,128)(2,1)S(1)}, bf16[8192,16]{0,1:T(8,128)(2,1)}, u32[]{:S(2)}) copy-start(bf16[8192,16]{0,1:T(8,128)(2,1)} %param.26) | copy-start | bytes 786436
  7.2 78.7 %copy-start.7 = (bf16[512,18]{0,1:T(8,128)(2,1)S(1)}, bf16[512,18]{0,1:T(8,128)(2,1)}, u32[]{:S(2)}) copy-start(bf16[512,18]{0,1:T(8,128)(2,1)} %param.24) | copy-start | bytes 55300
  79.2 12.0 all-to-all-start.3
  91.2 74.2 %all-to-all-start.2 = ((bf16[16,512,16]{1,2,0:T(8,128)(2,1)}), bf16[16,512,16]{1,2,0:T(8,128)(2,1)S(1)}, u32[]{:S(2)}, u32[]{:S(2)}) async-start(bf16[16,512,16]{1,2,0:T(8,128)(2,1)} %bitcast.96), calls=%async_computation.2 | async-start | bytes 524288 | tf_op jit(solution)/shard_map/all_to_all | solution.py:149
  94.8 809.6 %all-gather.10.cloned.1.call-start = ((), (), s32[]{:S(2)}) async-start(), calls=%async_computation.13 | async-start | bytes 5048320 | tf_op jit(solution)/shard_map/all_gather | solution.py:41
  103.4 66.2 %copy-start.3 = (bf16[16,2,8192]{2,1,0:T(2,128)(2,1)S(1)}, bf16[16,2,8192]{2,1,0:T(2,128)(2,1)}, u32[]{:S(2)}) copy-start(bf16[16,2,8192]{2,1,0:T(2,128)(2,1)} %param.23) | copy-start | bytes 1572868
  169.5 747.1 %all-gather.8.cloned.1.call-start = ((), (), s32[]{:S(2)}) async-start(), calls=%async_computation.10 | async-start | bytes 8912896 | tf_op jit(solution)/shard_map/all_gather | solution.py:153
  208.7 14.5 copy-start.12
  208.7 348.1 %copy-start.5 = (bf16[2,4096]{1,0:T(2,128)(2,1)S(1)}, bf16[2,4096]{1,0:T(2,128)(2,1)}, u32[]{:S(2)}) copy-start(bf16[2,4096]{1,0:T(2,128)(2,1)} %param.15) | copy-start | bytes 49156
  212.8 348.7 %copy-start.11 = (bf16[4,32]{1,0:T(4,128)(2,1)S(1)}, bf16[4,32]{1,0:T(4,128)(2,1)}, u32[]{:S(2)}) copy-start(bf16[4,32]{1,0:T(4,128)(2,1)} %param.19) | copy-start | bytes 772
  212.8 348.7 %copy-start.13 = (bf16[2,32]{1,0:T(2,128)(2,1)S(1)}, bf16[2,32]{1,0:T(2,128)(2,1)}, u32[]{:S(2)}) copy-start(bf16[2,32]{1,0:T(2,128)(2,1)} %param.20) | copy-start | bytes 388
  212.8 691.3 %copy-start.4 = (bf16[3,32,512]{2,1,0:T(8,128)(2,1)S(1)}, bf16[3,32,512]{2,1,0:T(8,128)(2,1)}, u32[]{:S(2)}) copy-start(bf16[3,32,512]{2,1,0:T(8,128)(2,1)} %param.16) | copy-start | bytes 294916
  558.0 346.2 %all-to-all-start = ((bf16[16,2,4096]{2,1,0:T(2,128)(2,1)}), bf16[16,2,4096]{2,1,0:T(2,128)(2,1)S(1)}, u32[]{:S(2)}, u32[]{:S(2)}) async-start(bf16[16,2,4096]{2,1,0:T(2,128)(2,1)} %broadcast_in_dim.24), calls=%async_computation | async-start | bytes 524288 | tf_op jit(solution)/shard_map/all_to_all | solution.py:23
  927.9 10.6 copy-start.9
  933.9 350.1 %copy-start.14 = (bf16[32]{0:T(256)(128)(2,1)S(1)}, bf16[32]{0:T(256)(128)(2,1)}, u32[]{:S(2)}) copy-start(bf16[32]{0:T(256)(128)(2,1)} %param.21) | copy-start | bytes 196
  933.9 448.8 %copy-start.8 = (s32[2,2]{1,0:T(2,128)S(1)}, s32[2,2]{1,0:T(2,128)}, u32[]{:S(2)}) copy-start(s32[2,2]{1,0:T(2,128)} %param.29) | copy-start | bytes 52
  934.9 464.2 %all-to-all-start.4 = ((bf16[16,32,288]{2,1,0:T(8,128)(2,1)}), bf16[16,32,288]{2,1,0:T(8,128)(2,1)S(1)}, u32[]{:S(2)}, u32[]{:S(2)}) async-start(bf16[16,32,288]{2,1,0:T(8,128)(2,1)} %broadcast_in_dim.25), calls=%async_computation.4 | async-start | bytes 786432 | tf_op jit(solution)/shard_map/all_to_all | solution.py:23
  1382.9 4.5 slice-start
  1392.6 6.9 copy-start.2
  1399.3 11.5 copy-start.1
  1405.3 371.3 %all-to-all-start.5 = ((bf16[16,2,4096]{2,1,0:T(2,128)(2,1)}), bf16[16,2,4096]{2,1,0:T(2,128)(2,1)S(1)}, u32[]{:S(2)}, u32[]{:S(2)}) async-start(bf16[16,2,4096]{2,1,0:T(2,128)(2,1)} %reshape.243), calls=%async_computation.5 | async-start | bytes 524288 | tf_op jit(solution)/shard_map/all_to_all | solution.py:60
  1430.9 17.7 copy-start.10
  1776.6 39.4 %all-to-all-start.7 = ((bf16[16,2,24576]{2,1,0:T(2,128)(2,1)}), bf16[16,2,24576]{2,1,0:T(2,128)(2,1)S(1)}, u32[]{:S(2)}, u32[]{:S(2)}) async-start(bf16[16,2,24576]{2,1,0:T(2,128)(2,1)} %reshape.277), calls=%async_computation.7 | async-start | bytes 3145728 | tf_op jit(solution)/shard_map/all_to_all | solution.py:140
  1815.0 38.2 %copy-start = (bf16[64,4097]{1,0:T(8,128)(2,1)}, bf16[64,4097]{1,0:T(8,128)(2,1)S(1)}, u32[]{:S(2)}) copy-start(bf16[64,4097]{1,0:T(8,128)(2,1)S(1)} %reshape.261) | copy-start | bytes 1573252
  1816.0 63.7 %all-to-all-start.6 = ((bf16[64,16,256]{2,0,1:T(8,128)(2,1)}), bf16[64,16,256]{2,0,1:T(8,128)(2,1)S(1)}, u32[]{:S(2)}, u32[]{:S(2)}) async-start(bf16[64,16,256]{2,0,1:T(8,128)(2,1)} %bitcast.95), calls=%async_computation.6 | async-start | bytes 1048576 | tf_op jit(solution)/shard_map/all_to_all | solution.py:227
  1841.0 89.4 %reduce-scatter.3.cloned.1.call-start = ((), (), s32[]{:S(2)}) async-start(), calls=%async_computation.11 | async-start | bytes 3932160 | tf_op jit(solution)/shard_map/reduce_scatter | solution.py:80
  1887.5 43.0 %slice-start.1 = ((bf16[3,32,512]{2,1,0:T(8,128)(2,1)}), bf16[2,32,512]{2,1,0:T(8,128)(2,1)S(1)}, s32[]{:S(2)}) async-start(bf16[3,32,512]{2,1,0:T(8,128)(2,1)} %param.16), calls=%async_computation.15 | async-start | bytes 131072 | tf_op jit(solution)/shard_map/slice | solution.py:172
  1891.4 73.2 %reduce-scatter.5.cloned.1.call-start = ((), (), s32[]{:S(2)}) async-start(), calls=%async_computation.12 | async-start | bytes 983040 | tf_op jit(solution)/shard_map/reduce_scatter | solution.py:80
Sparse Core Ops, SparseCore 0:
  169.6 81.2 all-gather.9
  253.9 117.8 all-gather.7
  1891.5 38.8 reduce-scatter.2
  1932.9 31.7 reduce-scatter.4
where the time goes:
time: 1980 us; the launch traced here: 1970 us
  blocking collectives  1500 us (76%)
  local copies, waits for them, and re-layouts  252 us (13%)
  waiting for transfers between devices  76.8 us (4%)
  other arithmetic  70.1 us (4%)
  starting transfers between devices  51.1 us (3%)
    all_gather x1, blocking collectives, shards(): lax.all_gather(decay_log, REP_TP, axis=1, tiled=True)  344 us
    all_gather x1, blocking collectives, in_one_piece(): out = lax.all_gather(both, axis, axis=dim, tiled=True)  342 us
    all_gather x1, blocking collectives, shards(): lax.all_gather(norm_gains, REP_TP, axis=1, tiled=True)  333 us
    all_gather x1, blocking collectives, shards(): lax.all_gather(router, REP_TP, axis=0, tiled=True)  328 us
    unnamed x1, blocking collectives  98.4 us
    unnamed x48, local copies, waits for them, and re-layouts  91.4 us
    reduce_scatter x2, waiting for transfers between devices, own_block(): blocks = lax.psum_scatter(blocks, axes[k], scatter_dimension=0, tiled=True)  71.6 us
    unnamed x3, other arithmetic  62.6 us
  transfers between devices with their start and end apart: 11, of which 3 were waited for; matrix products, arithmetic and copies ran while one was open for 11% of the time, Pallas kernels for 0%

commit v1 on v0

--- a/solution.py
+++ b/solution.py
@@ -111,7 +111,9 @@
     tp_count = lax.axis_size("tp")
     tp_index = lax.axis_index("tp")
     norm_gain, conv_taps, skip_rows, shift_full, decay_full, router_full = (
-        lax.all_gather(norm_gains, REP_TP, axis=1, tiled=True),
+        jnp.concatenate(
+            lax.all_to_all(jnp.stack([norm_gains] * lax.axis_size(REP_TP)), REP_TP, 0, 0), axis=1
+        ),
         *in_one_piece((conv_weight, conv_skip), REP_TP, 1, 0),
         lax.all_gather(step_bias, REP_TP, axis=0, tiled=True),
         lax.all_gather(decay_log, REP_TP, axis=1, tiled=True),

time: 1980 us -> 1660 us (0.84)
  blocking collectives: 1500 us -> 1160 us
    all_gather x1 -> x0, blocking collectives: 333 us -> none  [shards(): lax.all_gather(norm_gains, REP_TP, axis=1, tiled=True)]
    unnamed x48 -> x47, local copies, waits for them, and re-layouts: 91.4 us -> 91.3 us
  transfers between devices with their start and end apart: 11 -> 12, of which waited for: 3 -> 4; matrix products, arithmetic and copies ran while one was open for 11% -> 13% of each run, Pallas kernels for 0% -> 0%
where the time goes in v1:
time: 1660 us; the launch traced here: 1650 us
  blocking collectives  1160 us (70%)
  local copies, waits for them, and re-layouts  254 us (15%)
  waiting for transfers between devices  84.6 us (5%)
  other arithmetic  70.8 us (4%)
  starting transfers between devices  60 us (4%)
    all_gather x1, blocking collectives, shards(): lax.all_gather(decay_log, REP_TP, axis=1, tiled=True)  344 us
    all_gather x1, blocking collectives, in_one_piece(): out = lax.all_gather(both, axis, axis=dim, tiled=True)  337 us
    all_gather x1, blocking collectives, shards(): lax.all_gather(router, REP_TP, axis=0, tiled=True)  328 us
    unnamed x1, blocking collectives  99.5 us
    unnamed x47, local copies, waits for them, and re-layouts  91.3 us
    reduce_scatter x2, waiting for transfers between devices, own_block(): blocks = lax.psum_scatter(blocks, axes[k], scatter_dimension=0, tiled=True)  71.7 us
    unnamed x3, other arithmetic  62.6 us
    all_to_all x1, local copies, waits for them, and re-layouts, shards(): lax.all_to_all(step_proj.reshape(step_proj.shape[0], 1, 1, inner_all), 't...  62 us
  transfers between devices with their start and end apart: 12, of which 4 were waited for; matrix products, arithmetic and copies ran while one was open for 13% of the time, Pallas kernels for 0%

profile of v1, /device:TPU:2, one launch (start us, length us, event | category | flops | bytes accessed | tf_op | source)
XLA Modules:
  0.0 1653.9 jit_solution(902156170161684680)
XLA Ops:
  7.2 8.3 copy.128
  16.0 62.6 %reduce.20 = bf16[8192]{0:T(1024)(128)(2,1)S(1)} reduce(bf16[8192,1,1,1]{3,2,1,0:T(2,128)(2,1)} %bitcast.97, bf16[]{:T(256)} %broadcast.168), dimensions={1,2,3}, to_apply=%bitcast.70.reduce_sub_computation | reduce | bytes 32770
  79.2 5.9 all-to-all-start.4
  86.2 5.0 all-to-all-done.4
  91.2 3.5 all-to-all-start.3
  95.0 8.4 reshape.309
  103.4 62.0 %bitcast_reduce_fusion = bf16[8192]{0:T(1024)(128)(2,1)S(1)} fusion(bf16[8192,1,1,1]{3,2,1,0:T(2,128)(2,1)} %reshape.309), kind=kLoop, calls=%fused_computation.74 | loop fusion | bytes 32768 | tf_op jit(solution)/shard_map/all_to_all | solution.py:143
  165.4 2.0 copy.127
  167.4 1.3 reshape.260
  169.6 6.8 copy.122
  176.3 7.7 bitcast_bitcast_fusion
  184.0 5.8 reshape.310
  189.8 18.9 %all_to_all.97 = bf16[16,2,8192]{2,1,0:T(2,128)(2,1)S(1)} all-to-all(bf16[16,2,8192]{2,1,0:T(2,128)(2,1)S(1)} %reshape.310), channel_id=1, replica_groups=mesh['rep_0'=4,'rep_1'=4,'tp'=16] {'tp'}, dimensions={0} | all-to-all | bytes 1048576 | tf_op jit(solution)/shard_map/all_to_all | solution.py:135
  208.7 4.1 reshape.311
  212.8 10.3 copy.145
  223.9 8.9 all-to-all-start
  233.0 336.7 %all-gather.1 = bf16[256,32,6]{1,2,0:T(8,128)(2,1)S(1)} all-gather(bf16[1,32,6]{1,2,0:T(8,128)(2,1)S(1)} %maximum_bitcast_fusion.1), channel_id=1, replica_groups=mesh['rep_0'=4,'rep_1'=4,'tp'=16] {'rep_0','rep_1','tp'}, dimensions={0}, use_global_device_ids=true | all-gather | bytes 98688 | tf_op jit(solution)/shard_map/all_gather | solution.py:17
  572.2 3.5 all-to-all-start.1
  575.9 7.8 all-to-all-done.1
  583.8 5.1 reshape.276
  588.9 1.0 slice.100
  589.9 5.1 reshape.264
  596.1 11.7 copy.125
  607.8 6.0 fusion.26
  614.8 3.6 all-to-all-start.5
  618.4 343.8 %all-gather.2 = bf16[256,32,16]{1,2,0:T(8,128)(2,1)S(1)} all-gather(bf16[1,32,16]{1,2,0:T(8,128)(2,1)S(1)} %bitcast.117), channel_id=1, replica_groups=mesh['rep_0'=4,'rep_1'=4,'tp'=16] {'rep_0','rep_1','tp'}, dimensions={0}, use_global_device_ids=true | all-gather | bytes 263168 | tf_op jit(solution)/shard_map/all_gather | solution.py:119
  962.5 1.1 reshape.282
  963.9 99.5 %all-reduce = bf16[8192]{0:T(1024)(128)(2,1)S(1)} all-reduce(bf16[8192]{0:T(1024)(128)(2,1)S(1)} %dynamic-update-slice), channel_id=1, replica_groups=mesh['rep_0'=4,'rep_1'=4,'tp'=16] {'rep_0','rep_1','tp'}, use_global_device_ids=true, to_apply=%add | all-reduce | flops 8192 | bytes 32768
  1063.7 4.4 slice.107
  1068.2 5.1 copy.150
  1073.3 6.5 copy.132
  1080.2 1.5 multiply_reduce_fusion
  1081.6 3.5 convolution_convert_fusion
  1086.0 5.3 all-to-all-start.6
  1091.5 20.2 %copy.135 = bf16[16,2,2,12288]{0,2,1,3:T(2,128)(2,1)} copy(bf16[16,2,2,12288]{3,2,1,0:T(2,128)(2,1)S(1)} %copy-done.1) | data formatting | bytes 3145728 | tf_op args[13]
  1111.7 17.7 %reshape.312 = bf16[16,2,24576]{2,1,0:T(2,128)(2,1)} reshape(bf16[12288,2,2,16]{3,2,1,0:T(2,128)(2,1)} %bitcast.92) | data formatting | bytes 3145728
  1129.3 328.0 %all_gather.30 = bf16[4096,16]{1,0:T(8,128)(2,1)S(1)} all-gather(bf16[16,16]{1,0:T(8,128)(2,1)S(1)} %copy-done.10), channel_id=1, replica_groups=mesh['rep_0'=4,'rep_1'=4,'tp'=16] {'rep_0','rep_1','tp'}, dimensions={0}, use_global_device_ids=true | all-gather | bytes 131584 | tf_op jit(solution)/shard_map/all_gather | solution.py:120
  1457.4 3.9 all-to-all-start.8
  1463.4 32.2 %all-gather.3 = bf16[16,4,4097]{2,1,0:T(4,128)(2,1)S(1)} all-gather(bf16[1,4,4097]{2,1,0:T(4,128)(2,1)S(1)} %maximum_bitcast_fusion), channel_id=1, replica_groups=mesh['rep_0'=4,'rep_1'=4,'tp'=16] {'tp'}, dimensions={0}, use_global_device_ids=true | all-gather | bytes 557192 | tf_op jit(solution)/shard_map/all_gather | solution.py:69
  1496.9 25.0 %all-to-all-start.7 = ((bf16[64,16,256]{2,0,1:T(8,128)(2,1)}), bf16[64,16,256]{2,0,1:T(8,128)(2,1)S(1)}, u32[]{:S(2)}, u32[]{:S(2)}) async-start(bf16[64,16,256]{2,0,1:T(8,128)(2,1)} %bitcast.88), calls=%async_computation.7 | async-start | bytes 1048576 | tf_op jit(solution)/shard_map/all_to_all | solution.py:229
  1521.9 12.1 reshape.313
  1534.1 26.5 %copy.136 = bf16[16,2,2,16,768]{4,0,3,2,1:T(8,128)(2,1)S(1)} copy(bf16[16,2,2,16,768]{0,2,1,4,3:T(2,128)(2,1)} %bitcast.91) | data formatting | bytes 3145728 | tf_op jit(solution)/shard_map/all_to_all | solution.py:142
  1560.8 1.0 convert_bitcast_fusion
  1561.8 3.2 copy.138
  1565.1 3.3 convert_element_type.138
  1568.4 3.9 copy.139
  1572.3 39.0 %reduce-scatter.3.cloned.1.call-done = bf16[4,64,1536]{2,1,0:T(8,128)(2,1)} async-done(((bf16[16,64,1536]{2,1,0:T(8,128)(2,1)}), bf16[4,64,1536]{2,1,0:T(8,128)(2,1)}) %reduce-scatter.3.cloned.1.call-update) | async-done | bytes 786448 | tf_op jit(solution)/shard_map/reduce_scatter | solution.py:80
  1612.8 32.7 %reduce-scatter.5.cloned.1.call-done = bf16[1,64,1536]{2,1,0:T(8,128)(2,1)} async-done(((bf16[4,64,1536]{2,1,0:T(8,128)(2,1)}), bf16[1,64,1536]{2,1,0:T(8,128)(2,1)}) %reduce-scatter.5.cloned.1.call-update) | async-done | bytes 196624 | tf_op jit(solution)/shard_map/reduce_scatter | solution.py:80
  (117 shorter events, 18.1 us)
Async XLA Ops:
  7.2 78.0 %copy-start.6 = (bf16[8192,16]{0,1:T(8,128)(2,1)S(1)}, bf16[8192,16]{0,1:T(8,128)(2,1)}, u32[]{:S(2)}) copy-start(bf16[8192,16]{0,1:T(8,128)(2,1)} %param.26) | copy-start | bytes 786436
  7.2 78.7 %copy-start.7 = (bf16[512,18]{0,1:T(8,128)(2,1)S(1)}, bf16[512,18]{0,1:T(8,128)(2,1)}, u32[]{:S(2)}) copy-start(bf16[512,18]{0,1:T(8,128)(2,1)} %param.24) | copy-start | bytes 55300
  79.2 12.0 all-to-all-start.4
  91.2 74.2 %all-to-all-start.3 = ((bf16[16,512,16]{1,2,0:T(8,128)(2,1)}), bf16[16,512,16]{1,2,0:T(8,128)(2,1)S(1)}, u32[]{:S(2)}, u32[]{:S(2)}) async-start(bf16[16,512,16]{1,2,0:T(8,128)(2,1)} %bitcast.89), calls=%async_computation.3 | async-start | bytes 524288 | tf_op jit(solution)/shard_map/all_to_all | solution.py:151
  94.8 489.1 %all-gather.9.cloned.1.call-start = ((), (), s32[]{:S(2)}) async-start(), calls=%async_computation.14 | async-start | bytes 5048320 | tf_op jit(solution)/shard_map/all_gather | solution.py:41
  103.4 66.2 %copy-start.3 = (bf16[16,2,8192]{2,1,0:T(2,128)(2,1)S(1)}, bf16[16,2,8192]{2,1,0:T(2,128)(2,1)}, u32[]{:S(2)}) copy-start(bf16[16,2,8192]{2,1,0:T(2,128)(2,1)} %param.23) | copy-start | bytes 1572868
  169.5 426.5 %all-gather.7.cloned.1.call-start = ((), (), s32[]{:S(2)}) async-start(), calls=%async_computation.11 | async-start | bytes 8912896 | tf_op jit(solution)/shard_map/all_gather | solution.py:155
  208.7 14.5 copy-start.12
  208.7 24.2 %copy-start.11 = (bf16[4,32]{1,0:T(4,128)(2,1)S(1)}, bf16[4,32]{1,0:T(4,128)(2,1)}, u32[]{:S(2)}) copy-start(bf16[4,32]{1,0:T(4,128)(2,1)} %param.19) | copy-start | bytes 772
  208.7 24.2 %copy-start.13 = (bf16[2,32]{1,0:T(2,128)(2,1)S(1)}, bf16[2,32]{1,0:T(2,128)(2,1)}, u32[]{:S(2)}) copy-start(bf16[2,32]{1,0:T(2,128)(2,1)} %param.20) | copy-start | bytes 388
  208.7 24.2 %copy-start.5 = (bf16[2,4096]{1,0:T(2,128)(2,1)S(1)}, bf16[2,4096]{1,0:T(2,128)(2,1)}, u32[]{:S(2)}) copy-start(bf16[2,4096]{1,0:T(2,128)(2,1)} %param.15) | copy-start | bytes 49156
  212.8 363.0 %copy-start.4 = (bf16[3,32,512]{2,1,0:T(8,128)(2,1)S(1)}, bf16[3,32,512]{2,1,0:T(8,128)(2,1)}, u32[]{:S(2)}) copy-start(bf16[3,32,512]{2,1,0:T(8,128)(2,1)} %param.16) | copy-start | bytes 294916
  223.9 346.4 %all-to-all-start = ((bf16[256,2,16]{2,1,0:T(2,128)(2,1)}), bf16[256,2,16]{2,1,0:T(2,128)(2,1)S(1)}, u32[]{:S(2)}, u32[]{:S(2)}) async-start(bf16[256,2,16]{2,1,0:T(2,128)(2,1)} %stack.2), calls=%async_computation | async-start | bytes 262144 | tf_op jit(solution)/shard_map/all_to_all | solution.py:115
  572.2 11.5 all-to-all-start.1
  607.8 10.6 copy-start.9
  613.7 349.9 %copy-start.14 = (bf16[32]{0:T(256)(128)(2,1)S(1)}, bf16[32]{0:T(256)(128)(2,1)}, u32[]{:S(2)}) copy-start(bf16[32]{0:T(256)(128)(2,1)} %param.21) | copy-start | bytes 196
  613.8 449.7 %copy-start.8 = (s32[2,2]{1,0:T(2,128)S(1)}, s32[2,2]{1,0:T(2,128)}, u32[]{:S(2)}) copy-start(s32[2,2]{1,0:T(2,128)} %param.29) | copy-start | bytes 52
  614.8 465.0 %all-to-all-start.5 = ((bf16[16,32,288]{2,1,0:T(8,128)(2,1)}), bf16[16,32,288]{2,1,0:T(8,128)(2,1)S(1)}, u32[]{:S(2)}, u32[]{:S(2)}) async-start(bf16[16,32,288]{2,1,0:T(8,128)(2,1)} %broadcast_in_dim.25), calls=%async_computation.5 | async-start | bytes 786432 | tf_op jit(solution)/shard_map/all_to_all | solution.py:23
  1063.7 4.4 slice-start
  1073.3 6.9 copy-start.2
  1080.0 11.5 copy-start.1
  1086.0 371.4 %all-to-all-start.6 = ((bf16[16,2,4096]{2,1,0:T(2,128)(2,1)}), bf16[16,2,4096]{2,1,0:T(2,128)(2,1)S(1)}, u32[]{:S(2)}, u32[]{:S(2)}) async-start(bf16[16,2,4096]{2,1,0:T(2,128)(2,1)} %reshape.268), calls=%async_computation.6 | async-start | bytes 524288 | tf_op jit(solution)/shard_map/all_to_all | solution.py:60
  1111.7 17.7 %copy-start.10 = (bf16[16,16]{1,0:T(8,128)(2,1)S(1)}, bf16[16,16]{1,0:T(8,128)(2,1)}, u32[]{:S(2)}) copy-start(bf16[16,16]{1,0:T(8,128)(2,1)} %param.27) | copy-start | bytes 1540
  1457.4 39.4 %all-to-all-start.8 = ((bf16[16,2,24576]{2,1,0:T(2,128)(2,1)}), bf16[16,2,24576]{2,1,0:T(2,128)(2,1)S(1)}, u32[]{:S(2)}, u32[]{:S(2)}) async-start(bf16[16,2,24576]{2,1,0:T(2,128)(2,1)} %reshape.312), calls=%async_computation.8 | async-start | bytes 3145728 | tf_op jit(solution)/shard_map/all_to_all | solution.py:142
  1495.9 38.2 %copy-start = (bf16[64,4097]{1,0:T(8,128)(2,1)}, bf16[64,4097]{1,0:T(8,128)(2,1)S(1)}, u32[]{:S(2)}) copy-start(bf16[64,4097]{1,0:T(8,128)(2,1)S(1)} %reshape.284) | copy-start | bytes 1573252
  1496.9 63.7 %all-to-all-start.7 = ((bf16[64,16,256]{2,0,1:T(8,128)(2,1)}), bf16[64,16,256]{2,0,1:T(8,128)(2,1)S(1)}, u32[]{:S(2)}, u32[]{:S(2)}) async-start(bf16[64,16,256]{2,0,1:T(8,128)(2,1)} %bitcast.88), calls=%async_computation.7 | async-start | bytes 1048576 | tf_op jit(solution)/shard_map/all_to_all | solution.py:229
  1521.9 89.4 %reduce-scatter.3.cloned.1.call-start = ((), (), s32[]{:S(2)}) async-start(), calls=%async_computation.12 | async-start | bytes 3932160 | tf_op jit(solution)/shard_map/reduce_scatter | solution.py:80
  1568.4 43.0 %slice-start.1 = ((bf16[3,32,512]{2,1,0:T(8,128)(2,1)}), bf16[2,32,512]{2,1,0:T(8,128)(2,1)S(1)}, s32[]{:S(2)}) async-start(bf16[3,32,512]{2,1,0:T(8,128)(2,1)} %param.16), calls=%async_computation.16 | async-start | bytes 131072 | tf_op jit(solution)/shard_map/slice | solution.py:174
  1572.3 73.2 %reduce-scatter.5.cloned.1.call-start = ((), (), s32[]{:S(2)}) async-start(), calls=%async_computation.13 | async-start | bytes 983040 | tf_op jit(solution)/shard_map/reduce_scatter | solution.py:80
Sparse Core Ops, SparseCore 0:
  169.6 88.0 all-gather.8
  260.7 115.8 all-gather.6
  1572.4 38.8 reduce-scatter.2
  1613.7 31.7 reduce-scatter.4
